TPU v7x, 512 devices: a whole 4x4x16 slice. The times are simulated.
512 devices in a mesh: gx: 32 (over y, x, core), gy: 16 (over z).
Axes of the slice: x: 4, y: 4, z: 16, core: 2. Of those that a mesh axis runs over, the one named last changes fastest.
Arguments:
- patches: bfloat16 [256, 8192], P('gy', 'gx'), may hold values from -400 to 400, as said below
- norm_gain: bfloat16 [8192], P('gx'), may hold values from 0.099609375 to 1.8984375
- gate_weight: bfloat16 [8192, 28672], P('gx', 'gy'), may hold values from -0.0625 to 0.0625
- up_weight: bfloat16 [8192, 28672], P('gx', 'gy'), may hold values from -0.0625 to 0.0625
- down_weight: bfloat16 [28672, 8192], P('gy', 'gx'), may hold values from -0.03125 to 0.03125
Outputs:
- block_out: bfloat16 [256, 8192], P('gy', 'gx')
Inputs may be any that keep to these rules, and one draw needn't show every extreme that they name: `patches`: real-valued activations of a pooled encoder.
All inputs are finite; a program needn't handle non-finite values.
Results may differ from a plain program's by a relative error of at most 0.0065.
Values may be sent and summed in bfloat16 or wider, within the bound.
A program may use at most 64 MiB of HBM per device.

v0:
```python
import jax
import jax.numpy as jnp
from jax import lax
from jax.sharding import Mesh
from jax.sharding import PartitionSpec as P

GX = ("gx_0", "gx_1", "gx_2")


EPS = 1e-05


def sent_to_all(value, axis):
    copies = jnp.broadcast_to(value, (lax.axis_size(axis), *value.shape))
    return lax.all_to_all(copies, axis, split_axis=0, concat_axis=0, tiled=True)


def taken_together(value, axis):
    return sent_to_all(value, axis).sum(axis=0)


def in_order(pieces, dim):
    lengths = list(pieces.shape[1:])
    lengths[dim] *= pieces.shape[0]
    return jnp.moveaxis(pieces, 0, dim).reshape(lengths)


def gathered_copies(value, axis, dim):
    pieces = sent_to_all(value, axis)
    return in_order(pieces, dim)


def in_blocks(value, dim, devices):
    before, after = (value.shape[:dim], value.shape[dim + 1 :])
    return jnp.moveaxis(value.reshape(*before, devices, -1, *after), dim, 0)


def summed_on_arrival(value, axis, dim):
    pieces = in_blocks(value, dim, lax.axis_size(axis))
    arrived = lax.all_to_all(pieces, axis, split_axis=0, concat_axis=0, tiled=True)
    return arrived.sum(axis=0)


def sum_in_two_steps(value, axes, dim):
    far, near = axes
    pieces = in_blocks(value, dim, lax.axis_size(far))
    nearer = summed_on_arrival(pieces, near, dim + 1)
    arrived = lax.all_to_all(nearer, far, split_axis=0, concat_axis=0, tiled=True)
    return arrived.sum(axis=0)


def filled_up(lines, devices):
    spare = -len(lines) % devices
    return jnp.pad(lines, [(0, spare)] + [(0, 0)] * (lines.ndim - 1))


def whole_of(value, axes, dim):
    far, near = axes
    leading = sent_to_all(value, far)
    pieces = jnp.swapaxes(sent_to_all(leading, near), 0, 1)
    return in_order(pieces.reshape(-1, *value.shape), dim)


def sum_by_parts(value, axes):
    lines = value.reshape(-1, value.shape[-1])
    own = sum_in_two_steps(
        filled_up(lines, lax.axis_size(axes[0]) * lax.axis_size(axes[1])), axes, 0
    )
    whole = whole_of(own, axes, 0)
    return whole[: len(lines)].reshape(value.shape)


def swiglu(sums):
    return (jax.nn.silu(sums[:, 0]) * sums[:, 1]).astype(jnp.bfloat16)


def per_device(patches, norm_gain, gate_weight, up_weight, down_weight):
    values = patches.astype(jnp.float32)
    square_total = taken_together(jnp.sum(values * values, axis=1), GX)
    width = patches.shape[1] * lax.axis_size(GX)
    scale = lax.rsqrt(square_total / width + EPS)
    normed = (values * scale[:, None] * norm_gain.astype(jnp.float32)[None, :]).astype(jnp.bfloat16)
    whole = gathered_copies(normed, "gy", 0)
    gate = jnp.dot(whole, gate_weight, preferred_element_type=jnp.float32)
    up = jnp.dot(whole, up_weight, preferred_element_type=jnp.float32)
    sums = sum_by_parts(jnp.stack([gate, up], axis=1), (("gx_0", "gx_1"), "gx_2"))
    hidden = swiglu(sums)
    partial_value = jnp.dot(hidden, down_weight, preferred_element_type=jnp.float32)
    return summed_on_arrival(partial_value, "gy", 0).astype(jnp.bfloat16)


def solution(mesh):
    torus = Mesh(mesh.devices.reshape(4, 4, 2, mesh.shape["gy"]), ("gx_0", "gx_1", "gx_2", "gy"))
    in_specs = (P("gy", GX), P(GX), P(GX, "gy"), P(GX, "gy"), P("gy", GX))
    out_specs = P("gy", GX)
    return jax.shard_map(
        per_device, mesh=torus, in_specs=in_specs, out_specs=out_specs, check_vma=False
    )
```

profile of v0, /device:TPU:32, one launch (start us, length us, event | category | flops | bytes accessed | tf_op | source)
XLA Modules:
  0.0 175.5 jit_solution(8526050780610893110)
XLA Ops:
  0.0 0.9 fusion.2
  0.9 0.6 broadcast_in_dim.14
  1.6 7.3 %all-to-all-start = ((f32[32,1,16]{2,1,0:T(1,128)}), f32[32,1,16]{2,1,0:T(1,128)S(1)}, u32[]{:S(2)}, u32[]{:S(2)}) async-start(f32[32,1,16]{2,1,0:T(1,128)} %broadcast_in_dim.14), calls=%async_computation | async-start | bytes 32768 | tf_op jit(solution)/shard_map/all_to_all | solution.py:15
  8.9 0.7 convert_element_type.17
  9.5 6.7 %all-to-all-done = f32[32,1,16]{2,1,0:T(1,128)S(1)} async-done(((f32[32,1,16]{2,1,0:T(1,128)}), f32[32,1,16]{2,1,0:T(1,128)S(1)}, u32[]{:S(2)}, u32[]{:S(2)}) %all-to-all-start) | async-done | bytes 2080 | tf_op jit(solution)/shard_map/all_to_all | solution.py:15
  16.3 0.8 fusion.4
  17.1 29.3 %all_to_all.36 = bf16[16,16,256]{2,1,0:T(8,128)(2,1)S(1)} all-to-all(bf16[16,16,256]{2,1,0:T(8,128)(2,1)S(1)} %broadcast_in_dim.15), channel_id=1, replica_groups=mesh['gx_0'=4,'gx_1'=4,'gx_2'=2,'gy'=16] {'gy'}, dimensions={0} | all-to-all | bytes 262144 | tf_op jit(solution)/shard_map/all_to_all | solution.py:15
  46.8 0.4 convolution_bitcast_fusion.1
  47.5 4.6 %copy.14 = f32[256,2,1792]{2,1,0:T(2,128)} copy(f32[256,2,1792]{2,0,1:T(8,128)S(1)} %pad_maximum_fusion) | data formatting | bytes 7340032 | tf_op jit(solution)/shard_map/stack | solution.py:86
  52.1 5.6 %reshape_reshape.3 = f32[16,2,16,1792]{3,2,1,0:T(8,128)} reshape(f32[256,2,1792]{2,1,0:T(2,128)} %copy.14) | data formatting | bytes 7340032 | tf_op jit(solution)/shard_map/reshape;reshape | solution.py:35
  57.7 2.3 %copy.15 = f32[2,16,16,1792]{3,2,1,0:T(8,128)S(1)} copy(f32[2,16,16,1792]{3,2,0,1:T(8,128)} %bitcast.18) | data formatting | bytes 7340032 | tf_op jit(solution)/shard_map/transpose | solution.py:35
  60.0 7.7 %all_to_all.37 = f32[2,16,16,1792]{3,2,1,0:T(8,128)} all-to-all(f32[2,16,16,1792]{3,2,1,0:T(8,128)S(1)} %copy.15), channel_id=1, replica_groups=mesh['gx_0'=4,'gx_1'=4,'gx_2'=2,'gy'=16] {'gx_2'}, dimensions={0} | all-to-all | bytes 7340032 | tf_op jit(solution)/shard_map/all_to_all | solution.py:40
  67.7 2.5 %reduce_sum.47 = f32[16,16,1792]{2,1,0:T(8,128)S(1)} reduce(f32[2,16,16,1792]{3,2,1,0:T(8,128)} %all_to_all.37, f32[]{:T(128)} %constant.4.clone.1), dimensions={0}, to_apply=%region_2.3 | reduce | flops 458752 | bytes 5505028 | tf_op jit(solution)/shard_map/reduce_sum | solution.py:41
  70.2 29.6 %all_to_all.38 = f32[16,16,1792]{2,1,0:T(8,128)} all-to-all(f32[16,16,1792]{2,1,0:T(8,128)S(1)} %reduce_sum.47), channel_id=1, replica_groups=mesh['gx_0'=4,'gx_1'=4,'gx_2'=2,'gy'=16] {'gx_0','gx_1'}, dimensions={0} | all-to-all | bytes 3670016 | tf_op jit(solution)/shard_map/all_to_all | solution.py:48
  99.7 1.6 reduce_sum.48
  101.5 28.1 %all_to_all.39 = f32[16,16,1792]{2,1,0:T(8,128)S(1)} all-to-all(f32[16,16,1792]{2,1,0:T(8,128)S(1)} %broadcast_in_dim.16), channel_id=1, replica_groups=mesh['gx_0'=4,'gx_1'=4,'gx_2'=2,'gy'=16] {'gx_0','gx_1'}, dimensions={0} | all-to-all | bytes 3670016 | tf_op jit(solution)/shard_map/all_to_all | solution.py:15
  130.0 6.7 %all_to_all.40 = f32[2,16,16,1792]{3,2,1,0:T(8,128)S(1)} all-to-all(f32[2,16,16,1792]{3,2,1,0:T(8,128)S(1)} %broadcast_in_dim.17), channel_id=1, replica_groups=mesh['gx_0'=4,'gx_1'=4,'gx_2'=2,'gy'=16] {'gx_2'}, dimensions={0} | all-to-all | bytes 7340032 | tf_op jit(solution)/shard_map/all_to_all | solution.py:15
  136.7 2.0 %copy.16 = f32[16,2,16,1792]{3,2,1,0:T(8,128)} copy(f32[16,2,16,1792]{3,2,0,1:T(8,128)S(1)} %bitcast.19) | data formatting | bytes 7340032 | tf_op jit(solution)/shard_map/transpose | solution.py:60
  138.8 5.5 %reshape_reshape_reshape.3 = f32[256,2,1792]{2,1,0:T(2,128)} reshape(f32[16,2,16,1792]{3,2,1,0:T(8,128)} %copy.16) | data formatting | bytes 7340032 | tf_op jit(solution)/shard_map/reshape;reshape;reshape | solution.py:70
  144.2 6.3 %fusion.6 = (f32[256,1,1792]{2,1,0:T(1,128)S(1)}, f32[256,1,1792]{2,1,0:T(1,128)S(1)}) fusion(f32[256,2,1792]{2,1,0:T(2,128)} %reshape_reshape_reshape.3), kind=kLoop, calls=%fused_computation.13 | loop fusion | bytes 7340032 | tf_op jit(solution)/shard_map/slice | solution.py:74
  150.8 1.0 copy-done.2
  151.8 0.6 fusion
  152.5 22.5 %all_to_all.41 = f32[16,16,256]{2,1,0:T(8,128)S(1)} all-to-all(f32[16,16,256]{2,1,0:T(8,128)S(1)} %fusion), channel_id=1, replica_groups=mesh['gx_0'=4,'gx_1'=4,'gx_2'=2,'gy'=16] {'gy'}, dimensions={0} | all-to-all | bytes 524288 | tf_op jit(solution)/shard_map/all_to_all | solution.py:40
  174.9 0.6 reduce_sum.49
  (14 shorter events, 1.5 us)
Async XLA Ops:
  0.0 46.4 %copy-start = (bf16[256,1792]{1,0:T(8,128)(2,1)S(1)}, bf16[256,1792]{1,0:T(8,128)(2,1)}, u32[]{:S(2)}) copy-start(bf16[256,1792]{1,0:T(8,128)(2,1)} %param.8) | copy-start | bytes 2752516
  0.0 46.8 %copy-start.1 = (bf16[256,1792]{1,0:T(8,128)(2,1)S(1)}, bf16[256,1792]{1,0:T(8,128)(2,1)}, u32[]{:S(2)}) copy-start(bf16[256,1792]{1,0:T(8,128)(2,1)} %param.7) | copy-start | bytes 2752516
  1.6 14.7 %all-to-all-start = ((f32[32,1,16]{2,1,0:T(1,128)}), f32[32,1,16]{2,1,0:T(1,128)S(1)}, u32[]{:S(2)}, u32[]{:S(2)}) async-start(f32[32,1,16]{2,1,0:T(1,128)} %broadcast_in_dim.14), calls=%async_computation | async-start | bytes 32768 | tf_op jit(solution)/shard_map/all_to_all | solution.py:15
  150.6 1.2 copy-start.2
where the time goes:
time: 176 us
  blocking collectives  124 us (70%)
  local copies, waits for them, and re-layouts  28.8 us (16%)
  other arithmetic  7.36 us (4%)
  starting transfers between devices  7.32 us (4%)
  waiting for transfers between devices  6.72 us (4%)
    all_to_all x3, blocking collectives, sent_to_all(): return lax.all_to_all(copies, axis, split_axis=0, concat_axis=0, tiled=True)  64.1 us
    all_to_all x2, blocking collectives, summed_on_arrival(): lax.all_to_all(pieces, axis, split_axis=0, concat_axis=0, tiled=True)  30.2 us
    all_to_all x1, blocking collectives, sum_in_two_steps(): lax.all_to_all(nearer, far, split_axis=0, concat_axis=0, tiled=True)  29.6 us
    all_to_all x1, starting transfers between devices, sent_to_all(): return lax.all_to_all(copies, axis, split_axis=0, concat_axis=0, tiled=True)  7.32 us
    all_to_all x1, waiting for transfers between devices, sent_to_all(): return lax.all_to_all(copies, axis, split_axis=0, concat_axis=0, tiled=True)  6.72 us
    slice x1, local copies, waits for them, and re-layouts, swiglu(): return (jax.nn.silu(sums[:, 0]) * sums[:, 1]).astype(jnp.bfloat16)  6.31 us
    another operation x1, local copies, waits for them, and re-layouts, in_blocks(): return jnp.moveaxis(value.reshape(*before, devices, -1, *after), dim, 0)  5.57 us
    another operation x1, local copies, waits for them, and re-layouts, sum_by_parts(): return whole[:len(lines)].reshape(value.shape)  5.46 us
  transfers between devices with their start and end apart: 1, of which 1 were waited for; matrix products, arithmetic and copies ran while one was open for 0% of the time, Pallas kernels for 0%

commit v1 on v0

v1 whole, which is shorter than its diff:
```python
import functools

import jax
import jax.numpy as jnp
from jax import lax
from jax.experimental import pallas as pl
from jax.experimental.pallas import tpu as pltpu
from jax.sharding import Mesh
from jax.sharding import PartitionSpec as P

GX = ("gx_0", "gx_1", "gx_2")
EPS = 1e-05
MESH = pl.DeviceIdType.MESH

NZ = 16
TB = 16
DL = 256
FL = 1792
FH = FL // 2
NO = 16
GT = 128
OT = GT // NO
PW = FL + 128
NEAR = 4
HOME = 3


def place(rel):
    return (rel + HOME) % NZ


def kernel(
    x_hbm, gain_hbm, wg_hbm, wu_hbm, wd_hbm, out_ref,
    xb, gb, wgu, wd, pb, rb, hb, db, de, zs, zb,
    loc_sem, bar_w_send, bar_w_recv, x_send, x_recv, xd_send, xd_recv,
    p_send, p_recv, h_send, h_recv, d_send, d_recv, z_send, z_recv,
):
    y = lax.axis_index("gx_0")
    x = lax.axis_index("gx_1")
    c = lax.axis_index("gx_2")
    z = lax.axis_index("gy")
    other = 1 - c
    me = y * 4 + x
    partner = (y, x, other, z)

    def at_z(k):
        return (y, x, c, lax.rem(z + (k % NZ), NZ))

    def in_plane(d):
        return (lax.rem(y + d // 4, 4), lax.rem(x + d % 4, 4), c, z)

    own_half = pl.ds(pl.multiple_of(c * FH, 128), FH)
    other_half = pl.ds(pl.multiple_of(other * FH, 128), FH)
    own_d = pl.ds(pl.multiple_of(c * DL, 256), DL)
    loads = [
        pltpu.make_async_copy(x_hbm, xb.at[c, HOME * TB : (HOME + 1) * TB], loc_sem.at[0]),
        pltpu.make_async_copy(gain_hbm, gb.at[own_d], loc_sem.at[1]),
        pltpu.make_async_copy(wg_hbm.at[:, own_half], wgu.at[own_d, 0:FH], loc_sem.at[2]),
        pltpu.make_async_copy(wu_hbm.at[:, own_half], wgu.at[own_d, FH:FL], loc_sem.at[3]),
        pltpu.make_async_copy(wd_hbm.at[own_half, :], wd.at[:, own_d], loc_sem.at[4]),
    ]
    for copy in loads:
        copy.start()

    barrier = pltpu.get_barrier_semaphore()
    peers = [at_z(k) for k in range(-NEAR, NEAR + 1) if k != 0]
    peers += [in_plane(d) for d in range(1, NO)]
    peers += [partner]
    for peer in peers:
        pl.semaphore_signal(barrier, inc=1, device_id=peer, device_id_type=MESH)
    loads[0].wait()
    pl.semaphore_wait(barrier, len(peers))

    def block(rel):
        p = place(rel)
        return xb.at[c, p * TB : (p + 1) * TB]

    def send_x(src_rel, k, index):
        return pltpu.make_async_remote_copy(
            src_ref=block(src_rel),
            dst_ref=block(src_rel - k),
            send_sem=x_send.at[index],
            recv_sem=x_recv.at[(src_rel - k) % NZ],
            device_id=at_z(k),
            device_id_type=MESH,
        )

    def arrive_x(rel):
        pltpu.make_async_remote_copy(
            src_ref=block(rel),
            dst_ref=block(rel),
            send_sem=x_send.at[0],
            recv_sem=x_recv.at[rel % NZ],
            device_id=partner,
            device_id_type=MESH,
        ).wait_recv()

    x_copies = []
    for k in range(NEAR, 0, -1):
        for s in (k, -k):
            copy = send_x(0, s, len(x_copies))
            copy.start()
            x_copies.append(copy)

    w_copies = []
    for i, (src, dst) in enumerate(
        [
            (gain_hbm, gb.at[own_d]),
            (wg_hbm.at[:, other_half], wgu.at[own_d, 0:FH]),
            (wu_hbm.at[:, other_half], wgu.at[own_d, FH:FL]),
            (wd_hbm.at[other_half, :], wd.at[:, own_d]),
        ]
    ):
        copy = pltpu.make_async_remote_copy(
            src_ref=src,
            dst_ref=dst,
            send_sem=bar_w_send.at[i],
            recv_sem=bar_w_recv.at[i],
            device_id=partner,
            device_id_type=MESH,
        )
        copy.start()
        w_copies.append(copy)

    arrive_x(-NEAR)
    for k in range(NEAR, 0, -1):
        copy = send_x(-NEAR, k, len(x_copies))
        copy.start()
        x_copies.append(copy)
    arrive_x(NEAR)
    for k in range(NEAR - 1, 0, -1):
        copy = send_x(NEAR, -k, len(x_copies))
        copy.start()
        x_copies.append(copy)

    def to_partner(g):
        rows = slice(g * GT, (g + 1) * GT)
        return pltpu.make_async_remote_copy(
            src_ref=xb.at[c, rows],
            dst_ref=xb.at[c, rows],
            send_sem=xd_send.at[g],
            recv_sem=xd_recv.at[g],
            device_id=partner,
            device_id_type=MESH,
        )

    def gate_up(g):
        rows = slice(g * GT, (g + 1) * GT)
        acc = None
        squares = None
        for h in range(2):
            values = xb[h, rows, :].astype(jnp.float32)
            part = jnp.sum(values * values, axis=1, keepdims=True)
            squares = part if squares is None else squares + part
            scaled = values * gb[h * DL : (h + 1) * DL].astype(jnp.float32)[None, :]
            high = scaled.astype(jnp.bfloat16)
            low = (scaled - high.astype(jnp.float32)).astype(jnp.bfloat16)
            w = wgu[h * DL : (h + 1) * DL, :]
            for lhs in (high, low):
                part = jnp.dot(lhs, w, preferred_element_type=jnp.float32)
                acc = part if acc is None else acc + part
        pb[g, :, :, 0:FL] = acc.reshape(NO, OT, FL).astype(jnp.bfloat16)
        sq_high = squares.astype(jnp.bfloat16).astype(jnp.float32)
        sq_low = squares - sq_high
        lane = lax.broadcasted_iota(jnp.int32, (GT, 128), 1)
        lanes = jnp.where(lane == 0, sq_high, jnp.where(lane == 1, sq_low, 0.0))
        pb[g, :, :, FL:PW] = lanes.reshape(NO, OT, 128).astype(jnp.bfloat16)

    def send_parts(g):
        copies = []
        for d in (10, 6, 14, 9, 11, 2, 8, 5, 7, 13, 15, 1, 3, 4, 12):
            peer = in_plane(d)
            copy = pltpu.make_async_remote_copy(
                src_ref=pb.at[g, peer[0] * 4 + peer[1]],
                dst_ref=rb.at[g, d - 1],
                send_sem=p_send.at[g * NO + d],
                recv_sem=p_recv.at[g * NO + d],
                device_id=peer,
                device_id_type=MESH,
            )
            copy.start()
            copies.append(copy)
        return copies

    def hidden(g, copies):
        for copy in copies:
            copy.wait_recv()
        total = pb[g, me].astype(jnp.float32)
        for d in range(NO - 1):
            total = total + rb[g, d].astype(jnp.float32)
        mean_sq = jnp.sum(total[:, FL:PW], axis=1, keepdims=True) / (DL * 32)
        scale = lax.rsqrt(mean_sq + EPS)
        gate = total[:, 0:FH] * scale
        up = total[:, FH:FL] * scale
        hb[g, me] = (gate / (1.0 + jnp.exp(-gate)) * up).astype(jnp.bfloat16)

    def send_hidden(g):
        copies = []
        for d in (10, 6, 14, 9, 11, 2, 8, 5, 7, 13, 15, 1, 3, 4, 12):
            copy = pltpu.make_async_remote_copy(
                src_ref=hb.at[g, me],
                dst_ref=hb.at[g, me],
                send_sem=h_send.at[g * NO + d],
                recv_sem=h_recv.at[g * NO + d],
                device_id=in_plane(d),
                device_id_type=MESH,
            )
            copy.start()
            copies.append(copy)
        return copies

    def down(g, copies):
        for copy in copies:
            copy.wait_recv()
        lhs = hb[g].astype(jnp.float32).reshape(GT, FH).astype(jnp.bfloat16)
        part = jnp.dot(lhs, wd[...], preferred_element_type=jnp.float32)
        db[g, 0] = part[:, 0:DL]
        db[g, 1] = part[:, DL:]
        copy = pltpu.make_async_remote_copy(
            src_ref=db.at[g, other],
            dst_ref=de.at[g],
            send_sem=d_send.at[g],
            recv_sem=d_recv.at[g],
            device_id=partner,
            device_id_type=MESH,
        )
        copy.start()
        return copy

    def send_home(g, copy):
        copy.wait_recv()
        total = db[g, c] + de[g]
        zs[g * 8 : (g + 1) * 8] = total.reshape(8, TB, DL).astype(jnp.bfloat16)
        copies = []
        rels = [r for r in range(-7, 9) if place(r) // 8 == g and r != 0]
        for r in sorted(rels, key=lambda r: -abs(r)):
            copy = pltpu.make_async_remote_copy(
                src_ref=zs.at[place(r)],
                dst_ref=zb.at[(-r) % NZ],
                send_sem=z_send.at[r % NZ],
                recv_sem=z_recv.at[(-r) % NZ],
                device_id=at_z(r),
                device_id_type=MESH,
            )
            copy.start()
            copies.append(copy)
        return copies

    for r in range(-HOME, NEAR):
        if r != 0:
            arrive_x(r)
    d_copies = [to_partner(0), to_partner(1)]
    d_copies[0].start()
    for copy in loads[1:]:
        copy.wait()
    for copy in w_copies:
        copy.wait_recv()
    d_copies[0].wait_recv()
    gate_up(0)
    parts = [send_parts(0)]

    for r in range(NEAR + 1, NEAR + 8):
        arrive_x(r)
    d_copies[1].start()
    d_copies[1].wait_recv()
    gate_up(1)
    parts.append(send_parts(1))

    hiddens = []
    for g in range(2):
        hidden(g, parts[g])
        hiddens.append(send_hidden(g))

    downs = []
    homes = []
    for g in range(2):
        downs.append(down(g, hiddens[g]))
    for g in range(2):
        homes += send_home(g, downs[g])

    total = zs[HOME].astype(jnp.float32)
    for r in range(1, NZ):
        pltpu.make_async_remote_copy(
            src_ref=zb.at[r],
            dst_ref=zb.at[r],
            send_sem=z_send.at[0],
            recv_sem=z_recv.at[r],
            device_id=partner,
            device_id_type=MESH,
        ).wait_recv()
    for r in range(1, NZ):
        total = total + zb[r].astype(jnp.float32)
    out_ref[...] = total.astype(jnp.bfloat16)

    for copy in x_copies + w_copies + d_copies + parts[0] + parts[1] + hiddens[0] + hiddens[1] + downs + homes:
        copy.wait_send()


def per_device(patches, norm_gain, gate_weight, up_weight, down_weight):
    bf16, f32 = jnp.bfloat16, jnp.float32
    dma = pltpu.SemaphoreType.DMA
    return pl.pallas_call(
        kernel,
        out_shape=jax.ShapeDtypeStruct((TB, DL), bf16),
        in_specs=[pl.BlockSpec(memory_space=pltpu.HBM)] * 5,
        out_specs=pl.BlockSpec(memory_space=pltpu.VMEM),
        scratch_shapes=[
            pltpu.VMEM((2, NZ * TB, DL), bf16),
            pltpu.VMEM((2 * DL,), bf16),
            pltpu.VMEM((2 * DL, FL), bf16),
            pltpu.VMEM((FH, 2 * DL), bf16),
            pltpu.VMEM((2, NO, OT, PW), bf16),
            pltpu.VMEM((2, NO - 1, OT, PW), bf16),
            pltpu.VMEM((2, NO, OT, FH), bf16),
            pltpu.VMEM((2, 2, GT, DL), f32),
            pltpu.VMEM((2, GT, DL), f32),
            pltpu.VMEM((NZ, TB, DL), bf16),
            pltpu.VMEM((NZ, TB, DL), bf16),
            dma((5,)),
            dma((4,)), dma((4,)),
            dma((15,)), dma((NZ,)),
            dma((2,)), dma((2,)),
            dma((2 * NO,)), dma((2 * NO,)),
            dma((2 * NO,)), dma((2 * NO,)),
            dma((2,)), dma((2,)),
            dma((NZ,)), dma((NZ,)),
        ],
        compiler_params=pltpu.CompilerParams(
            collective_id=0, has_side_effects=True, vmem_limit_bytes=67043328
        ),
    )(patches, norm_gain, gate_weight, up_weight, down_weight)


def solution(mesh):
    torus = Mesh(mesh.devices.reshape(4, 4, 2, mesh.shape["gy"]), ("gx_0", "gx_1", "gx_2", "gy"))
    in_specs = (P("gy", GX), P(GX), P(GX, "gy"), P(GX, "gy"), P("gy", GX))
    out_specs = P("gy", GX)
    return jax.shard_map(
        per_device, mesh=torus, in_specs=in_specs, out_specs=out_specs, check_vma=False
    )
```

time: 176 us -> 54.9 us (0.31)
  the two profiles are of different devices: /device:TPU:32 before, /device:TPU:1 now
where the time goes in v1:
time: 54.9 us; the launch traced here: 54.6 us
  Pallas kernels  53.3 us (97%)
  local copies, waits for them, and re-layouts  1.3 us (2%)
    pallas_call x1, Pallas kernels, per_device(): pl.pallas_call(kernel, out_shape=jax.ShapeDtypeStruct((TB, DL), bf16), in...  53.3 us
    unnamed x1, local copies, waits for them, and re-layouts  1.3 us

profile of v1, /device:TPU:1, one launch (start us, length us, event | category | flops | bytes accessed | tf_op | source)
XLA Modules:
  0.0 54.6 jit_solution(9099013902185986628)
XLA Ops:
  0.0 53.3 %shard_map.55 = bf16[16,256]{1,0:T(8,128)(2,1)} custom-call(bf16[16,256]{1,0:T(8,128)(2,1)} %x_hbm.1, bf16[256]{0:T(256)(128)(2,1)} %gain_hbm.1, bf16[256,1792]{1,0:T(8,128)(2,1)} %wg_hbm.1, bf16[256,1792]{1,0:T(8,128)(2,1)} %wu_hbm.1, bf16[1792,256]{1,0:T(8,128)(2,1)} %wd_hbm.1), custom_call_target="tpu_custom_call" | custom-call | tf_op jit(solution)/shard_map/pallas_call | solution.py:302
  53.4 1.3 %copy.7 = bf16[16,256]{1,0:T(8,128)(2,1)} copy(bf16[16,256]{1,0:T(8,128)(2,1)} %shard_map.55) | data formatting | bytes 16384
